TPU v7x, 32 devices: a whole 2x2x4 slice. The times are simulated.
32 devices in a mesh: gx: 4 (over y, core), gy: 4 (over z), gz: 2 (over x).
Axes of the slice: x: 2, y: 2, z: 4, core: 2. Of those that a mesh axis runs over, the one named last changes fastest.
Arguments:
- stream: bfloat16 [8192, 8192], P(('gx', 'gy', 'gz')), may hold values from -4 to 4
- segment_ids: int32 [8192], P(('gx', 'gy', 'gz')), may hold values from 0 to 8191, as said below
- positions: int32 [8192], P(('gx', 'gy', 'gz')), may hold values from 0 to 255, as said below
- norm_gain: bfloat16 [1, 8192], P(None, ('gx', 'gy', 'gz')), may hold values from 0.099609375 to 1.8984375
- q_weight: bfloat16 [1, 8192, 512], P(None, ('gx', 'gy', 'gz')), as said below
- k_weight: bfloat16 [1, 8192, 128], P(None, ('gx', 'gy', 'gz')), as said below
- v_weight: bfloat16 [1, 8192, 128], P(None, ('gx', 'gy', 'gz')), may hold values from -0.0625 to 0.0625
- o_weight: bfloat16 [1, 512, 8192], P(None, None, ('gx', 'gy', 'gz')), may hold values from -0.25 to 0.25
Outputs:
- result: bfloat16 [8192, 8192], P(('gx', 'gy', 'gz'))
Inputs may be any that keep to these rules, and one draw needn't show every extreme that they name: `segment_ids`: each token's id is the index of its document's first token, so ids never fall along the tokens; every document lies inside one aligned block of 256 tokens, every block starts a new document, and the last token is a document of its own. `positions`: counts from 0 at a document's first token and rises by one per token. `q_weight`: A projection scaled by its fan-in. `k_weight`: A projection scaled by its fan-in.
All inputs are finite; a program needn't handle non-finite values.
Results may differ from a plain program's by a relative error of at most 0.0064.
Values may be sent and summed in bfloat16 or wider, within the bound.
A program may use at most 128 MiB of HBM per device.

v0:
```python
import math
import jax
import jax.numpy as jnp
from jax import lax
from jax.sharding import PartitionSpec as P


def rotate(values, positions):
    width = values.shape[-1]
    half = width // 2
    freqs = jnp.exp(-math.log(500000.0) * jnp.arange(half, dtype=jnp.float32) * 2.0 / width)
    angles = positions.astype(jnp.float32)[:, None] * freqs[None, :]
    cosine = jnp.concatenate([jnp.cos(angles), jnp.cos(angles)], -1)[:, None, :]
    sine = jnp.concatenate([jnp.sin(angles), jnp.sin(angles)], -1)[:, None, :]
    turned = jnp.concatenate([-values[..., half:], values[..., :half]], -1)
    return values * cosine + turned * sine


def attend(queries, keys, values, segment_ids, positions):
    count = queries.shape[0]
    scores = jnp.einsum(
        "thd,sd->hts", queries, keys, preferred_element_type=jnp.float32
    ) / math.sqrt(keys.shape[-1])
    allowed = (segment_ids[:, None] == segment_ids[None, :]) & (
        positions[None, :] <= positions[:, None]
    )
    scores = jnp.where(allowed[None], scores, -1e30)
    peak = jnp.max(scores, -1, keepdims=True)
    expd = jnp.exp(scores - peak)
    probs = (expd / jnp.sum(expd, -1, keepdims=True)).astype(jnp.bfloat16)
    mixed = jnp.einsum("hts,sd->thd", probs, values, preferred_element_type=jnp.float32)
    return mixed.astype(jnp.bfloat16).reshape(count, -1)


def body(stream, segment_ids, positions, norm_gain, q_weight, k_weight, v_weight, o_weight):
    count = stream.shape[0]
    head_size = k_weight.shape[2]
    current = stream
    widened = lax.optimization_barrier(current).astype(jnp.float32)
    inverse = lax.rsqrt(jnp.mean(widened * widened, -1, keepdims=True) + 1e-05)
    scaled = widened * inverse
    inner = (
        lax.all_gather(norm_gain[0], "gz", axis=0, tiled=True),
        lax.all_gather(q_weight[0], "gz", axis=0, tiled=True),
        lax.all_gather(k_weight[0], "gz", axis=0, tiled=True),
        lax.all_gather(v_weight[0], "gz", axis=0, tiled=True),
    )
    middle = (
        lax.all_gather(inner[0], "gy", axis=0, tiled=True),
        lax.all_gather(inner[1], "gy", axis=0, tiled=True),
        lax.all_gather(inner[2], "gy", axis=0, tiled=True),
        lax.all_gather(inner[3], "gy", axis=0, tiled=True),
    )
    gain_piece = lax.all_gather(middle[0], "gx", axis=0, tiled=True)
    query_piece = lax.all_gather(middle[1], "gx", axis=0, tiled=True)
    key_piece = lax.all_gather(middle[2], "gx", axis=0, tiled=True)
    value_piece = lax.all_gather(middle[3], "gx", axis=0, tiled=True)
    normed = (scaled * gain_piece.astype(jnp.float32)[None, :]).astype(jnp.bfloat16)
    query_raw = jnp.dot(normed, query_piece, preferred_element_type=jnp.float32)
    key_raw = jnp.dot(normed, key_piece, preferred_element_type=jnp.float32)
    value_raw = jnp.dot(normed, value_piece, preferred_element_type=jnp.float32)
    queries = rotate(query_raw.reshape(count, -1, head_size), positions).astype(jnp.bfloat16)
    keys = rotate(key_raw[:, None, :], positions)[:, 0, :].astype(jnp.bfloat16)
    values = value_raw.astype(jnp.bfloat16)
    mixed = attend(queries, keys, values, segment_ids, positions)
    inner_cols = lax.all_gather(o_weight[0], "gz", axis=1, tiled=True)
    middle_cols = lax.all_gather(inner_cols, "gy", axis=1, tiled=True)
    branch = jnp.dot(
        mixed,
        lax.all_gather(middle_cols, "gx", axis=1, tiled=True),
        preferred_element_type=jnp.float32,
    )
    current = (widened + branch).astype(jnp.bfloat16)
    return current


def solution(mesh):
    in_specs = (
        P(("gx", "gy", "gz"), None),
        P(("gx", "gy", "gz")),
        P(("gx", "gy", "gz")),
        P(None, ("gx", "gy", "gz")),
        P(None, ("gx", "gy", "gz"), None),
        P(None, ("gx", "gy", "gz"), None),
        P(None, ("gx", "gy", "gz"), None),
        P(None, None, ("gx", "gy", "gz")),
    )
    out_specs = P(("gx", "gy", "gz"), None)
    return jax.shard_map(body, mesh=mesh, in_specs=in_specs, out_specs=out_specs, check_vma=False)
```

profile of v0, /device:TPU:0, one launch (start us, length us, event | category | flops | bytes accessed | tf_op | source)
XLA Modules:
  0.0 307.4 jit_solution(744721059821343803)
XLA Ops:
  6.5 0.0 all-gather.26.cloned.1.call-start
  6.5 12.0 %all-gather.9 = bf16[1,512,512]{2,1,0:T(8,128)(2,1)} all-gather(bf16[1,256,512]{2,1,0:T(8,128)(2,1)} %param.12), channel_id=11, replica_groups=mesh['gx'=4,'gy'=4,'gz'=2] {'gz'}, dimensions={1}, use_global_device_ids=true | all-gather | bytes 786432 | tf_op jit(solution)/shard_map/all_gather | solution.py:44
  18.6 0.0 all-gather.26.cloned.1.call-update
  18.6 0.0 copy-start.3
  18.6 0.0 copy-start.1
  18.6 0.0 all-gather.30.cloned.1.call-start
  18.7 8.5 %all-gather.12 = bf16[1,512,512]{2,1,0:T(8,128)(2,1)} all-gather(bf16[1,512,256]{2,1,0:T(8,128)(2,1)} %param.15), channel_id=14, replica_groups=mesh['gx'=4,'gy'=4,'gz'=2] {'gz'}, dimensions={2}, use_global_device_ids=true | all-gather | bytes 786432 | tf_op jit(solution)/shard_map/all_gather | solution.py:66
  27.1 0.0 all-gather.30.cloned.1.call-update
  27.2 0.0 all-gather.24.cloned.1.call-start
  27.2 5.2 %all-gather.6 = bf16[1,512,128]{2,1,0:T(8,128)(2,1)S(1)} all-gather(bf16[1,256,128]{2,1,0:T(8,128)(2,1)} %param.13), channel_id=8, replica_groups=mesh['gx'=4,'gy'=4,'gz'=2] {'gz'}, dimensions={1}, use_global_device_ids=true | all-gather | bytes 196608 | tf_op jit(solution)/shard_map/all_gather | solution.py:45
  32.4 23.9 %all-gather.7 = bf16[1,2048,128]{2,1,0:T(8,128)(2,1)} all-gather(bf16[1,512,128]{2,1,0:T(8,128)(2,1)S(1)} %all-gather.6), channel_id=9, replica_groups=mesh['gx'=4,'gy'=4,'gz'=2] {'gy'}, dimensions={1}, use_global_device_ids=true | all-gather | bytes 655360 | tf_op jit(solution)/shard_map/all_gather | solution.py:51
  56.2 0.0 all-gather.24.cloned.1.call-update
  56.2 0.0 all-gather.28.cloned.1.call-start
  56.3 16.9 %all-gather.26.cloned.1.call-done = bf16[1,2048,512]{2,1,0:T(8,128)(2,1)} async-done(((bf16[1,512,512]{2,1,0:T(8,128)(2,1)}), bf16[1,2048,512]{2,1,0:T(8,128)(2,1)}) %all-gather.26.cloned.1.call-update) | async-done | bytes 2097168 | tf_op jit(solution)/shard_map/all_gather | solution.py:50
  73.2 0.0 all-gather.28.cloned.1.call-update
  73.2 0.0 copy-start.2
  73.2 0.0 all-gather.22.cloned.1.call-start
  73.2 0.0 copy-done
  73.3 4.9 %all-gather.3 = bf16[1,512,128]{2,1,0:T(8,128)(2,1)S(1)} all-gather(bf16[1,256,128]{2,1,0:T(8,128)(2,1)S(1)} %copy-done), channel_id=5, replica_groups=mesh['gx'=4,'gy'=4,'gz'=2] {'gz'}, dimensions={1}, use_global_device_ids=true | all-gather | bytes 196608 | tf_op jit(solution)/shard_map/all_gather | solution.py:46
  78.2 20.2 %all-gather.4 = bf16[1,2048,128]{2,1,0:T(8,128)(2,1)} all-gather(bf16[1,512,128]{2,1,0:T(8,128)(2,1)S(1)} %all-gather.3), channel_id=6, replica_groups=mesh['gx'=4,'gy'=4,'gz'=2] {'gy'}, dimensions={1}, use_global_device_ids=true | all-gather | bytes 655360 | tf_op jit(solution)/shard_map/all_gather | solution.py:52
  98.4 0.0 all-gather.22.cloned.1.call-update
  98.4 0.0 all-gather.32.cloned.1.call-start
  98.4 26.2 %all-gather.30.cloned.1.call-done = bf16[1,512,2048]{2,1,0:T(8,128)(2,1)} async-done(((bf16[1,512,512]{2,1,0:T(8,128)(2,1)}), bf16[1,512,2048]{2,1,0:T(8,128)(2,1)}) %all-gather.30.cloned.1.call-update) | async-done | bytes 2097168 | tf_op jit(solution)/shard_map/all_gather | solution.py:67
  124.7 0.0 all-gather.32.cloned.1.call-update
  124.7 0.0 copy-done.3
  124.7 4.2 %all-gather = bf16[1,512]{1,0:T(2,128)(2,1)S(1)} all-gather(bf16[1,256]{1,0:T(2,128)(2,1)S(1)} %copy-done.3), channel_id=2, replica_groups=mesh['gx'=4,'gy'=4,'gz'=2] {'gz'}, dimensions={1}, use_global_device_ids=true | all-gather | bytes 1536 | tf_op jit(solution)/shard_map/all_gather | solution.py:43
  128.9 11.9 %all-gather.1 = bf16[1,2048]{1,0:T(2,128)(2,1)S(1)} all-gather(bf16[1,512]{1,0:T(2,128)(2,1)S(1)} %all-gather), channel_id=3, replica_groups=mesh['gx'=4,'gy'=4,'gz'=2] {'gy'}, dimensions={1}, use_global_device_ids=true | all-gather | bytes 5120 | tf_op jit(solution)/shard_map/all_gather | solution.py:49
  140.9 5.5 %all-gather.2 = bf16[1,8192]{1,0:T(2,128)(2,1)S(1)} all-gather(bf16[1,2048]{1,0:T(2,128)(2,1)S(1)} %all-gather.1), channel_id=4, replica_groups=mesh['gx'=4,'gy'=4,'gz'=2] {'gx'}, dimensions={1}, use_global_device_ids=true | all-gather | bytes 20480 | tf_op jit(solution)/shard_map/all_gather | solution.py:54
  146.4 0.0 copy-done.1
  146.4 3.1 %fusion.2 = f32[256]{0:T(256)S(1)} fusion(bf16[256,8192]{1,0:T(8,128)(2,1)} %param.8), kind=kLoop, calls=%fused_computation.5 | loop fusion | flops 6291200 | bytes 4195328 | tf_op jit(solution)/shard_map/reduce_sum | solution.py:40
  149.6 0.0 copy-done.2
  149.6 0.1 compare_and_fusion
  149.7 0.3 multiply_cosine_fusion
  150.0 0.0 all-gather.24.cloned.1.call-done
  150.1 4.6 %fusion.8 = f32[256,128]{0,1:T(8,128)S(1)} fusion(bf16[1,8192,128]{2,1,0:T(8,128)(2,1)} %all-gather.24.cloned.1.call-done, bf16[256,8192]{1,0:T(8,128)(2,1)} %param.8, f32[8192]{0:T(1024)S(1)} %bitcast.83, f32[256]{0:T(256)S(1)} %add_rsqrt_fusion), kind=kOutput, calls=%fused_computation.11 | convolution fusion | flops 545259520 | bytes 6456320 | tf_op jit(solution)/shard_map/dot_general | solution.py:60
  154.7 0.1 copy.10
  154.8 0.1 copy.9
  154.9 52.9 %all-gather.28.cloned.1.call-done = bf16[1,8192,512]{2,1,0:T(8,128)(2,1)} async-done(((bf16[1,2048,512]{2,1,0:T(8,128)(2,1)}), bf16[1,8192,512]{2,1,0:T(8,128)(2,1)}) %all-gather.28.cloned.1.call-update) | async-done | bytes 8388624 | tf_op jit(solution)/shard_map/all_gather | solution.py:55
  207.9 7.0 %fusion.6 = f32[256,512]{1,0:T(8,128)S(1)} fusion(bf16[1,8192,512]{2,1,0:T(8,128)(2,1)} %all-gather.28.cloned.1.call-done, bf16[256,8192]{1,0:T(8,128)(2,1)} %param.8, f32[8192]{0:T(1024)S(1)} %bitcast.84, f32[256]{0:T(256)S(1)} %add_rsqrt_fusion), kind=kOutput, calls=%fused_computation.9 | convolution fusion | flops 2155872256 | bytes 13140992 | tf_op jit(solution)/shard_map/dot_general | solution.py:59
  214.9 0.2 reshape.93
  215.1 0.3 slice_negate_fusion
  215.4 0.4 maximum_multiply_fusion
  215.8 0.1 mul.85
  215.9 0.5 fusion.44
  216.4 15.4 %all-gather.22.cloned.1.call-done = bf16[1,8192,128]{2,1,0:T(8,128)(2,1)} async-done(((bf16[1,2048,128]{2,1,0:T(8,128)(2,1)}), bf16[1,8192,128]{2,1,0:T(8,128)(2,1)}) %all-gather.22.cloned.1.call-update) | async-done | bytes 2097168 | tf_op jit(solution)/shard_map/all_gather | solution.py:57
  231.9 4.7 %convolution_convert_fusion = bf16[128,4,256]{2,0,1:T(8,128)(2,1)S(1)} fusion(bf16[1,8192,128]{2,1,0:T(8,128)(2,1)} %all-gather.22.cloned.1.call-done, f32[4,256,256]{1,2,0:T(8,128)S(1)} %get-tuple-element.15, f32[4,256]{1,0:T(4,128)S(1)} %get-tuple-element.14, bf16[256,8192]{1,0:T(8,128)(2,1)} %param.8, f32[8192]{0:T(1024)S(1)} %bitcast.85, ...), kind=kOutput, calls=%fused_computation.20 | convolution fusion | flops 613056512 | bytes 7640064 | tf_op jit(solution)/shard_map/hts,sd->thd/dot_general | solution.py:31
  236.5 55.0 %all-gather.32.cloned.1.call-done = bf16[1,512,8192]{2,1,0:T(8,128)(2,1)} async-done(((bf16[1,512,2048]{2,1,0:T(8,128)(2,1)}), bf16[1,512,8192]{2,1,0:T(8,128)(2,1)}) %all-gather.32.cloned.1.call-update) | async-done | bytes 8388624 | tf_op jit(solution)/shard_map/all_gather | solution.py:70
  291.6 9.0 %fusion.1 = bf16[256,8192]{1,0:T(8,128)(2,1)} fusion(bf16[256,512]{0,1:T(8,128)(2,1)S(1)} %bitcast.82, bf16[256,8192]{1,0:T(8,128)(2,1)} %param.8, bf16[1,512,8192]{2,1,0:T(8,128)(2,1)} %all-gather.32.cloned.1.call-done), kind=kOutput, calls=%fused_computation.4 | convolution fusion | flops 2153775104 | bytes 17039360 | tf_op jit(solution)/shard_map/dot_general | solution.py:68
  (7 shorter events, 0.1 us)
Async XLA Ops:
  6.5 66.7 %copy-start = (bf16[1,256,128]{2,1,0:T(8,128)(2,1)S(1)}, bf16[1,256,128]{2,1,0:T(8,128)(2,1)}, u32[]{:S(2)}) copy-start(bf16[1,256,128]{2,1,0:T(8,128)(2,1)} %param.14) | copy-start | bytes 196612
  6.5 66.6 %all-gather.26.cloned.1.call-start = ((), (), s32[]{:S(2)}) async-start(), calls=%async_computation.2 | async-start | bytes 2621440 | tf_op jit(solution)/shard_map/all_gather | solution.py:50
  18.6 106.1 %copy-start.3 = (bf16[1,256]{1,0:T(2,128)(2,1)S(1)}, bf16[1,256]{1,0:T(2,128)(2,1)}, u32[]{:S(2)}) copy-start(bf16[1,256]{1,0:T(2,128)(2,1)} %param.11) | copy-start | bytes 1540
  18.6 127.8 %copy-start.1 = (s32[256]{0:T(256)S(1)}, s32[256]{0:T(256)}, u32[]{:S(2)}) copy-start(s32[256]{0:T(256)} %param.10) | copy-start | bytes 3076
  18.6 106.0 %all-gather.30.cloned.1.call-start = ((), (), s32[]{:S(2)}) async-start(), calls=%async_computation.4 | async-start | bytes 2621440 | tf_op jit(solution)/shard_map/all_gather | solution.py:67
  27.2 122.9 %all-gather.24.cloned.1.call-start = ((), (), s32[]{:S(2)}) async-start(), calls=%async_computation.1 | async-start | bytes 2621440 | tf_op jit(solution)/shard_map/all_gather | solution.py:56
  56.2 151.6 %all-gather.28.cloned.1.call-start = ((), (), s32[]{:S(2)}) async-start(), calls=%async_computation.3 | async-start | bytes 10485760 | tf_op jit(solution)/shard_map/all_gather | solution.py:55
  73.2 76.4 %copy-start.2 = (s32[256]{0:T(256)S(1)}, s32[256]{0:T(256)}, u32[]{:S(2)}) copy-start(s32[256]{0:T(256)} %param.9) | copy-start | bytes 3076
  73.2 158.7 %all-gather.22.cloned.1.call-start = ((), (), s32[]{:S(2)}) async-start(), calls=%async_computation | async-start | bytes 2621440 | tf_op jit(solution)/shard_map/all_gather | solution.py:57
  98.4 193.2 %all-gather.32.cloned.1.call-start = ((), (), s32[]{:S(2)}) async-start(), calls=%async_computation.5 | async-start | bytes 10485760 | tf_op jit(solution)/shard_map/all_gather | solution.py:70
Sparse Core Ops, SparseCore 0:
  18.7 54.3 all-gather.25
  74.7 49.8 all-gather.29
  126.2 21.8 all-gather.23
  149.6 58.2 all-gather.27
  209.3 22.5 all-gather.21
  233.3 58.2 all-gather.31
where the time goes:
time: 308 us; the launch traced here: 307 us
  waiting for transfers between devices  167 us (54%)
  blocking collectives  96.3 us (31%)
  matrix products  25.9 us (8%)
  between operations  13.6 us (4%)
  other arithmetic  4.37 us (1%)
    all_gather x1, waiting for transfers between devices, body(): lax.all_gather(middle_cols, 'gx', axis=1, tiled=True)  55 us
    all_gather x1, waiting for transfers between devices, body(): query_piece = lax.all_gather(middle[1], 'gx', axis=0, tiled=True)  52.9 us
    all_gather x1, waiting for transfers between devices, body(): middle_cols = lax.all_gather(inner_cols, 'gy', axis=1, tiled=True)  26.2 us
    all_gather x1, blocking collectives, body(): lax.all_gather(inner[2], 'gy', axis=0, tiled=True)  23.9 us
    all_gather x1, blocking collectives, body(): lax.all_gather(inner[3], 'gy', axis=0, tiled=True)  20.2 us
    all_gather x1, waiting for transfers between devices, body(): lax.all_gather(inner[1], 'gy', axis=0, tiled=True)  16.9 us
    all_gather x1, waiting for transfers between devices, body(): value_piece = lax.all_gather(middle[3], 'gx', axis=0, tiled=True)  15.4 us
    all_gather x1, blocking collectives, body(): lax.all_gather(q_weight[0], 'gz', axis=0, tiled=True)  12 us
  transfers between devices with their start and end apart: 6, of which 5 were waited for; matrix products, arithmetic and copies ran while one was open for 7% of the time, Pallas kernels for 0%

commit v1 on v0

--- a/solution.py
+++ b/solution.py
@@ -64,7 +64,12 @@
     values = value_raw.astype(jnp.bfloat16)
     mixed = attend(queries, keys, values, segment_ids, positions)
     inner_cols = lax.all_gather(o_weight[0], "gz", axis=1, tiled=True)
-    middle_cols = lax.all_gather(inner_cols, "gy", axis=1, tiled=True)
+    ring = [inner_cols]
+    for hop in range(3):
+        ring.append(lax.ppermute(ring[-1], "gy", [(dev, (dev + 1) % 4) for dev in range(4)]))
+    middle_cols = jnp.roll(
+        jnp.concatenate(ring[::-1], axis=1), (lax.axis_index("gy") + 1) * ring[0].shape[1], axis=1
+    )
     branch = jnp.dot(
         mixed,
         lax.all_gather(middle_cols, "gx", axis=1, tiled=True),

time: 308 us -> 253 us (0.82)
  waiting for transfers between devices: 167 us -> 116 us
  blocking collectives: 96.3 us -> 89.8 us
    all_gather x1, waiting for transfers between devices: 52.9 us -> 0.02 us  [body(): query_piece = lax.all_gather(middle[1], 'gx', axis=0, tiled=True)]
    ppermute x0 -> x3, waiting for transfers between devices: none -> 35.3 us  [body(): lax.ppermute(ring[-1], 'gy', [(dev, (dev + 1) % 4) for dev in range(4)])]
    all_gather x1 -> x0, waiting for transfers between devices: 26.2 us -> none  [body(): middle_cols = lax.all_gather(inner_cols, 'gy', axis=1, tiled=True)]
    all_gather x1, waiting for transfers between devices: 15.4 us -> 1.45 us  [body(): value_piece = lax.all_gather(middle[3], 'gx', axis=0, tiled=True)]
    all_gather x1, waiting for transfers between devices: 16.9 us -> 23.8 us  [body(): lax.all_gather(inner[1], 'gy', axis=0, tiled=True)]
    all_gather x1, blocking collectives: 20.2 us -> 16.3 us  [body(): lax.all_gather(inner[3], 'gy', axis=0, tiled=True)]
  transfers between devices with their start and end apart: 6 -> 8, of which waited for: 5 -> 6; matrix products, arithmetic and copies ran while one was open for 7% -> 10% of each run, Pallas kernels for 0% -> 0%
where the time goes in v1:
time: 253 us
  waiting for transfers between devices  116 us (46%)
  blocking collectives  89.8 us (35%)
  matrix products  26.1 us (10%)
  between operations  13.4 us (5%)
  other arithmetic  4.38 us (2%)
  local copies, waits for them, and re-layouts  2.61 us (1%)
    all_gather x1, waiting for transfers between devices, body(): lax.all_gather(middle_cols, 'gx', axis=1, tiled=True)  55 us
    ppermute x3, waiting for transfers between devices, body(): lax.ppermute(ring[-1], 'gy', [(dev, (dev + 1) % 4) for dev in range(4)])  35.3 us
    all_gather x1, waiting for transfers between devices, body(): lax.all_gather(inner[1], 'gy', axis=0, tiled=True)  23.8 us
    all_gather x1, blocking collectives, body(): lax.all_gather(inner[2], 'gy', axis=0, tiled=True)  23.1 us
    all_gather x1, blocking collectives, body(): lax.all_gather(inner[3], 'gy', axis=0, tiled=True)  16.3 us
    all_gather x1, blocking collectives, body(): lax.all_gather(q_weight[0], 'gz', axis=0, tiled=True)  12 us
    all_gather x1, blocking collectives, body(): lax.all_gather(inner[0], 'gy', axis=0, tiled=True)  11.9 us
    dot_general x1, matrix products, body(): jnp.dot(mixed, lax.all_gather(middle_cols, 'gx', axis=1, tiled=True), pre...  9.02 us
  transfers between devices with their start and end apart: 8, of which 6 were waited for; matrix products, arithmetic and copies ran while one was open for 10% of the time, Pallas kernels for 0%

profile of v1, /device:TPU:0, one launch (start us, length us, event | category | flops | bytes accessed | tf_op | source)
XLA Modules:
  0.0 253.1 jit_solution(4556272814398298820)
XLA Ops:
  6.5 12.0 %all-gather.9 = bf16[1,512,512]{2,1,0:T(8,128)(2,1)} all-gather(bf16[1,256,512]{2,1,0:T(8,128)(2,1)} %param.12), channel_id=11, replica_groups=mesh['gx'=4,'gy'=4,'gz'=2] {'gz'}, dimensions={1}, use_global_device_ids=true | all-gather | bytes 786432 | tf_op jit(solution)/shard_map/all_gather | solution.py:44
  18.6 0.0 all-gather.25.cloned.1.call-update
  18.6 0.0 all-gather.23.cloned.1.call-start
  18.6 5.1 %all-gather.6 = bf16[1,512,128]{2,1,0:T(8,128)(2,1)S(1)} all-gather(bf16[1,256,128]{2,1,0:T(8,128)(2,1)} %param.13), channel_id=8, replica_groups=mesh['gx'=4,'gy'=4,'gz'=2] {'gz'}, dimensions={1}, use_global_device_ids=true | all-gather | bytes 196608 | tf_op jit(solution)/shard_map/all_gather | solution.py:45
  23.8 23.1 %all-gather.7 = bf16[1,2048,128]{2,1,0:T(8,128)(2,1)} all-gather(bf16[1,512,128]{2,1,0:T(8,128)(2,1)S(1)} %all-gather.6), channel_id=9, replica_groups=mesh['gx'=4,'gy'=4,'gz'=2] {'gy'}, dimensions={1}, use_global_device_ids=true | all-gather | bytes 655360 | tf_op jit(solution)/shard_map/all_gather | solution.py:51
  46.9 0.0 all-gather.23.cloned.1.call-update
  46.9 0.0 all-gather.27.cloned.1.call-start
  47.0 23.8 %all-gather.25.cloned.1.call-done = bf16[1,2048,512]{2,1,0:T(8,128)(2,1)} async-done(((bf16[1,512,512]{2,1,0:T(8,128)(2,1)}), bf16[1,2048,512]{2,1,0:T(8,128)(2,1)}) %all-gather.25.cloned.1.call-update) | async-done | bytes 2097168 | tf_op jit(solution)/shard_map/all_gather | solution.py:50
  70.8 0.0 all-gather.21.cloned.1.call-start
  70.8 4.9 %all-gather.3 = bf16[1,512,128]{2,1,0:T(8,128)(2,1)S(1)} all-gather(bf16[1,256,128]{2,1,0:T(8,128)(2,1)S(1)} %copy-done.1), channel_id=5, replica_groups=mesh['gx'=4,'gy'=4,'gz'=2] {'gz'}, dimensions={1}, use_global_device_ids=true | all-gather | bytes 196608 | tf_op jit(solution)/shard_map/all_gather | solution.py:46
  75.8 16.3 %all-gather.4 = bf16[1,2048,128]{2,1,0:T(8,128)(2,1)} all-gather(bf16[1,512,128]{2,1,0:T(8,128)(2,1)S(1)} %all-gather.3), channel_id=6, replica_groups=mesh['gx'=4,'gy'=4,'gz'=2] {'gy'}, dimensions={1}, use_global_device_ids=true | all-gather | bytes 655360 | tf_op jit(solution)/shard_map/all_gather | solution.py:52
  92.0 0.0 all-gather.21.cloned.1.call-update
  92.1 0.0 all-gather.19.cloned.1.call-start
  92.1 7.0 %all-gather.12 = bf16[1,512,512]{2,1,0:T(8,128)(2,1)S(1)} all-gather(bf16[1,512,256]{2,1,0:T(8,128)(2,1)S(1)} %copy-done), channel_id=14, replica_groups=mesh['gx'=4,'gy'=4,'gz'=2] {'gz'}, dimensions={2}, use_global_device_ids=true | all-gather | bytes 786432 | tf_op jit(solution)/shard_map/all_gather | solution.py:66
  99.2 0.9 collective-permute-start
  100.1 11.2 %collective-permute-done = bf16[512,512]{1,0:T(8,128)(2,1)S(1)} collective-permute-done((bf16[512,512]{1,0:T(8,128)(2,1)S(1)}, bf16[512,512]{1,0:T(8,128)(2,1)S(1)}, u32[]{:S(2)}, u32[]{:S(2)}) %collective-permute-start) | collective-permute-done | bytes 524320 | tf_op jit(solution)/shard_map/ppermute | solution.py:69
  111.3 12.8 %collective-permute-done.1 = bf16[512,512]{1,0:T(8,128)(2,1)S(1)} collective-permute-done((bf16[512,512]{1,0:T(8,128)(2,1)S(1)}, bf16[512,512]{1,0:T(8,128)(2,1)S(1)}, u32[]{:S(2)}, u32[]{:S(2)}) %collective-permute-start.1) | collective-permute-done | bytes 524320 | tf_op jit(solution)/shard_map/ppermute | solution.py:69
  124.0 11.3 %collective-permute-done.2 = bf16[512,512]{1,0:T(8,128)(2,1)S(1)} collective-permute-done((bf16[512,512]{1,0:T(8,128)(2,1)S(1)}, bf16[512,512]{1,0:T(8,128)(2,1)S(1)}, u32[]{:S(2)}, u32[]{:S(2)}) %collective-permute-start.2) | collective-permute-done | bytes 524320 | tf_op jit(solution)/shard_map/ppermute | solution.py:69
  135.4 0.1 constant_dynamic-update-slice_fusion.7
  135.4 0.1 constant_dynamic-update-slice_fusion.6
  135.5 0.1 constant_dynamic-update-slice_fusion.5
  135.6 0.1 constant_dynamic-update-slice_fusion.4
  135.7 0.1 constant_dynamic-update-slice_fusion.3
  135.7 0.1 constant_dynamic-update-slice_fusion.2
  135.9 0.1 constant_dynamic-update-slice_fusion.1
  135.9 0.1 constant_dynamic-update-slice_fusion
  136.0 1.6 constant_dynamic-slice_fusion
  137.6 4.2 %all-gather = bf16[1,512]{1,0:T(2,128)(2,1)S(1)} all-gather(bf16[1,256]{1,0:T(2,128)(2,1)S(1)} %copy-done.4), channel_id=2, replica_groups=mesh['gx'=4,'gy'=4,'gz'=2] {'gz'}, dimensions={1}, use_global_device_ids=true | all-gather | bytes 1536 | tf_op jit(solution)/shard_map/all_gather | solution.py:43
  141.9 11.9 %all-gather.1 = bf16[1,2048]{1,0:T(2,128)(2,1)S(1)} all-gather(bf16[1,512]{1,0:T(2,128)(2,1)S(1)} %all-gather), channel_id=3, replica_groups=mesh['gx'=4,'gy'=4,'gz'=2] {'gy'}, dimensions={1}, use_global_device_ids=true | all-gather | bytes 5120 | tf_op jit(solution)/shard_map/all_gather | solution.py:49
  153.8 5.2 %all-gather.2 = bf16[1,8192]{1,0:T(2,128)(2,1)S(1)} all-gather(bf16[1,2048]{1,0:T(2,128)(2,1)S(1)} %all-gather.1), channel_id=4, replica_groups=mesh['gx'=4,'gy'=4,'gz'=2] {'gx'}, dimensions={1}, use_global_device_ids=true | all-gather | bytes 20480 | tf_op jit(solution)/shard_map/all_gather | solution.py:54
  159.0 3.1 %fusion.2 = f32[256]{0:T(256)S(1)} fusion(bf16[256,8192]{1,0:T(8,128)(2,1)} %param.8), kind=kLoop, calls=%fused_computation.5 | loop fusion | flops 6291200 | bytes 4195328 | tf_op jit(solution)/shard_map/reduce_sum | solution.py:40
  162.2 0.1 compare_and_fusion
  162.3 0.3 multiply_cosine_fusion
  162.6 0.0 all-gather.23.cloned.1.call-done
  162.7 4.8 %fusion.7 = f32[256,128]{0,1:T(8,128)S(1)} fusion(bf16[1,8192,128]{2,1,0:T(8,128)(2,1)} %all-gather.23.cloned.1.call-done, bf16[256,8192]{1,0:T(8,128)(2,1)} %param.8, f32[8192]{0:T(1024)S(1)} %bitcast.85, f32[256]{0:T(256)S(1)} %add_rsqrt_fusion), kind=kOutput, calls=%fused_computation.10 | convolution fusion | flops 545259520 | bytes 6456320 | tf_op jit(solution)/shard_map/dot_general | solution.py:60
  167.6 0.1 copy.10
  167.7 0.1 copy.9
  167.8 0.0 all-gather.27.cloned.1.call-done
  167.8 7.1 %fusion.5 = f32[256,512]{1,0:T(8,128)S(1)} fusion(bf16[1,8192,512]{2,1,0:T(8,128)(2,1)} %all-gather.27.cloned.1.call-done, bf16[256,8192]{1,0:T(8,128)(2,1)} %param.8, f32[8192]{0:T(1024)S(1)} %bitcast.86, f32[256]{0:T(256)S(1)} %add_rsqrt_fusion), kind=kOutput, calls=%fused_computation.8 | convolution fusion | flops 2155872256 | bytes 13140992 | tf_op jit(solution)/shard_map/dot_general | solution.py:59
  174.9 0.2 reshape.93
  175.1 0.3 slice_negate_fusion
  175.4 0.4 maximum_multiply_fusion
  175.8 0.1 mul.88
  175.9 0.5 fusion.43
  176.4 1.4 all-gather.21.cloned.1.call-done
  177.9 4.7 %convolution_convert_fusion = bf16[128,4,256]{2,0,1:T(8,128)(2,1)S(1)} fusion(bf16[1,8192,128]{2,1,0:T(8,128)(2,1)} %all-gather.21.cloned.1.call-done, f32[4,256,256]{1,2,0:T(8,128)S(1)} %get-tuple-element.15, f32[4,256]{1,0:T(4,128)S(1)} %get-tuple-element.14, bf16[256,8192]{1,0:T(8,128)(2,1)} %param.8, f32[8192]{0:T(1024)S(1)} %bitcast.87, ...), kind=kOutput, calls=%fused_computation.19 | convolution fusion | flops 613056512 | bytes 7640064 | tf_op jit(solution)/shard_map/hts,sd->thd/dot_general | solution.py:31
  182.6 55.0 %all-gather.19.cloned.1.call-done = bf16[512,8192]{1,0:T(8,128)(2,1)} async-done(((bf16[512,2048]{1,0:T(8,128)(2,1)}), bf16[512,8192]{1,0:T(8,128)(2,1)}) %all-gather.19.cloned.1.call-update) | async-done | bytes 8388624 | tf_op jit(solution)/shard_map/all_gather | solution.py:75
  237.6 9.0 %fusion.1 = bf16[256,8192]{1,0:T(8,128)(2,1)} fusion(bf16[256,512]{0,1:T(8,128)(2,1)S(1)} %bitcast.84, bf16[512,8192]{1,0:T(8,128)(2,1)} %all-gather.19.cloned.1.call-done, bf16[256,8192]{1,0:T(8,128)(2,1)} %param.8), kind=kOutput, calls=%fused_computation.4 | convolution fusion | flops 2153775104 | bytes 17039360 | tf_op jit(solution)/shard_map/dot_general | solution.py:73
  (21 shorter events, 0.2 us)
Async XLA Ops:
  6.5 64.3 %copy-start.1 = (bf16[1,256,128]{2,1,0:T(8,128)(2,1)S(1)}, bf16[1,256,128]{2,1,0:T(8,128)(2,1)}, u32[]{:S(2)}) copy-start(bf16[1,256,128]{2,1,0:T(8,128)(2,1)} %param.14) | copy-start | bytes 196612
  6.5 85.6 %copy-start = (bf16[1,512,256]{2,1,0:T(8,128)(2,1)S(1)}, bf16[1,512,256]{2,1,0:T(8,128)(2,1)}, u32[]{:S(2)}) copy-start(bf16[1,512,256]{2,1,0:T(8,128)(2,1)} %param.15) | copy-start | bytes 786436
  6.5 64.2 %all-gather.25.cloned.1.call-start = ((), (), s32[]{:S(2)}) async-start(), calls=%async_computation.3 | async-start | bytes 2621440 | tf_op jit(solution)/shard_map/all_gather | solution.py:50
  18.6 144.1 %all-gather.23.cloned.1.call-start = ((), (), s32[]{:S(2)}) async-start(), calls=%async_computation.2 | async-start | bytes 2621440 | tf_op jit(solution)/shard_map/all_gather | solution.py:56
  46.9 120.9 %all-gather.27.cloned.1.call-start = ((), (), s32[]{:S(2)}) async-start(), calls=%async_computation.4 | async-start | bytes 10485760 | tf_op jit(solution)/shard_map/all_gather | solution.py:55
  70.8 107.1 %all-gather.21.cloned.1.call-start = ((), (), s32[]{:S(2)}) async-start(), calls=%async_computation.1 | async-start | bytes 2621440 | tf_op jit(solution)/shard_map/all_gather | solution.py:57
  92.1 145.5 %all-gather.19.cloned.1.call-start = ((), (), s32[]{:S(2)}) async-start(), calls=%async_computation | async-start | bytes 10485760 | tf_op jit(solution)/shard_map/all_gather | solution.py:75
  99.2 12.1 %collective-permute-start = (bf16[512,512]{1,0:T(8,128)(2,1)S(1)}, bf16[512,512]{1,0:T(8,128)(2,1)S(1)}, u32[]{:S(2)}, u32[]{:S(2)}) collective-permute-start(bf16[512,512]{1,0:T(8,128)(2,1)S(1)} %bitcast.80), channel_id=1, source_target_pairs={{0,2},{2,4},{4,6},{6,0},{1,3},{3,5},{5,7},{7,1},{8,10},{10,12},{12... | collective-permute-start | bytes 1572872 | tf_op jit(solution)/shard_map/ppermute | solution.py:69
  111.3 12.8 %collective-permute-start.1 = (bf16[512,512]{1,0:T(8,128)(2,1)S(1)}, bf16[512,512]{1,0:T(8,128)(2,1)S(1)}, u32[]{:S(2)}, u32[]{:S(2)}) collective-permute-start(bf16[512,512]{1,0:T(8,128)(2,1)S(1)} %collective-permute-done), channel_id=1, source_target_pairs={{0,2},{2,4},{4,6},{6,0},{1,3},{3,5},{5,7},{7,1},{8,10},{10,12},{12... | collective-permute-start | bytes 1572872 | tf_op jit(solution)/shard_map/ppermute | solution.py:69
  124.0 11.3 %collective-permute-start.2 = (bf16[512,512]{1,0:T(8,128)(2,1)S(1)}, bf16[512,512]{1,0:T(8,128)(2,1)S(1)}, u32[]{:S(2)}, u32[]{:S(2)}) collective-permute-start(bf16[512,512]{1,0:T(8,128)(2,1)S(1)} %collective-permute-done.1), channel_id=1, source_target_pairs={{0,2},{2,4},{4,6},{6,0},{1,3},{3,5},{5,7},{7,1},{8,10},{10,12},{12... | collective-permute-start | bytes 1572872 | tf_op jit(solution)/shard_map/ppermute | solution.py:69
  135.8 1.8 copy-start.2
  135.8 1.8 copy-start.4
  137.6 24.6 %copy-start.3 = (s32[256]{0:T(256)S(1)}, s32[256]{0:T(256)}, u32[]{:S(2)}) copy-start(s32[256]{0:T(256)} %param.9) | copy-start | bytes 3076
Sparse Core Ops, SparseCore 0:
  18.7 51.9 all-gather.24
  72.3 21.6 all-gather.22
  95.6 58.2 all-gather.26
  155.3 22.5 all-gather.20
  179.3 58.2 all-gather.18
